TPU v7x, 256 devices: a 8x8x2 block of a 8x8x16 slice. The times are simulated.
256 devices in a mesh: groups: 2 (over z), steps: 128 (over y, x, core).
Axes of the slice: x: 8, y: 8, z: 2, core: 2. Of those that a mesh axis runs over, the one named last changes fastest.
The devices are a block of a 8x8x16 slice.
Arguments:
- states: float32 [256, 4, 4096], P(('groups', 'steps')), parts along dimension 0, may hold values from -6 to 6
- t_sched: int32 [514], P('groups'), parts along dimension 0, may hold values from 0 to 999, as said below
- advances: int32 [4], P('groups'), parts along dimension 0, may hold values from 1 to 128, as said below
- in_weight: bfloat16 [320, 4], replicated, may hold values from -3 to 3
- time_weight: float32 [320, 320], replicated, may hold values from -0.3125 to 0.3125
- mid_weight: bfloat16 [320, 320], replicated, may hold values from -0.3125 to 0.3125
- out_weight: bfloat16 [4, 320], replicated, may hold values from -0.3125 to 0.3125
Outputs:
- final_states: float32 [256, 4, 4096], P(('groups', 'steps')), parts along dimension 0
- errors: float32 [4, 4, 128], P('groups', None, 'steps'), parts along dimension 0
There are 2 independent parts, one for each index of `groups`. A program takes and returns all parts, laid end to end along the dimension named above; an argument that names none is the same for every part. Nothing has to cross between parts.
Inputs may be any that keep to these rules, and one draw needn't show every extreme that they name: `t_sched`: strictly decreasing. Some round advances by exactly 128.
All inputs are finite; a program needn't handle non-finite values.
Results may differ from a plain program's by a relative error of at most 0.0024.
Values sent between devices are 32-bit elements; how exact they have to be, the bound alone decides.
No kernel may reach another device: no remote copies, remote signals or barrier semaphores. Data moves between devices by JAX's collectives and lax.ppermute only.
A program may use at most 64 MiB of HBM per device.

v0:
```python
import math
import jax
import jax.numpy as jnp
from jax import lax
from jax.sharding import Mesh
from jax.sharding import PartitionSpec as P

TSTEPS = 1000
ITERS = 4
ROUNDS = 2
STEPS = ("steps_0", "steps_1", "steps_2")
GROUPS_STEPS = ("groups", "steps_0", "steps_1", "steps_2")


def neutral_like(value, identity):
    return jnp.zeros_like(value) + jnp.asarray(identity, value.dtype)


def entering(value, axes, combine, identity):
    before = start = neutral_like(value, identity)
    so_far = value
    for axis in reversed(axes):
        devices, place = (lax.axis_size(axis), lax.axis_index(axis))
        pieces = lax.all_gather(so_far, axis)
        inside, so_far = (start, start)
        for k in range(devices):
            passed = k < place
            so_far = combine(so_far, pieces[k])
            inside = jnp.where(passed, so_far, inside)
        before = combine(inside, before)
    return before


def alpha_table():
    levels = jnp.arange(TSTEPS, dtype=jnp.float32)
    low = math.sqrt(0.00085)
    high = math.sqrt(0.012)
    betas = (low + (high - low) * levels / (TSTEPS - 1)) ** 2
    return jnp.exp(jnp.cumsum(jnp.log1p(-betas)))


def time_features(stamp, width):
    halfwidth = width // 2
    freqs = jnp.exp(-math.log(10000.0) * jnp.arange(halfwidth, dtype=jnp.float32) / halfwidth)
    angles = stamp.astype(jnp.float32) * freqs
    return jnp.concatenate([jnp.cos(angles), jnp.sin(angles)])


def lookup(alphas, stamp):
    levels = jnp.arange(alphas.shape[0], dtype=jnp.int32)
    return jnp.sum(jnp.where(levels == stamp, alphas, 0.0))


def denoise(state, embed, in_weight, mid_weight, out_weight):
    pre = (
        jnp.dot(in_weight, state.astype(jnp.bfloat16), preferred_element_type=jnp.float32)
        + embed[:, None]
    )
    hidden_one = jax.nn.silu(pre).astype(jnp.bfloat16)
    mixed = jnp.dot(mid_weight, hidden_one, preferred_element_type=jnp.float32)
    hidden_two = (jax.nn.silu(mixed) + pre).astype(jnp.bfloat16)
    return jnp.dot(out_weight, hidden_two, preferred_element_type=jnp.float32)


def add_terms(earlier, later):
    return earlier + later


def shards(states, t_sched, advances, in_weight, time_weight, mid_weight, out_weight):
    window = lax.axis_size(STEPS)
    own_index = lax.axis_index(STEPS)
    alphas = alpha_table()
    current = states
    window_start = jnp.int32(0)
    error_rows = []
    for round_no in range(ROUNDS):
        stamp_now = lax.dynamic_slice_in_dim(t_sched, window_start + own_index, 1)[0]
        stamp_next = lax.dynamic_slice_in_dim(t_sched, window_start + own_index + 1, 1)[0]
        alpha_now = lookup(alphas, stamp_now)
        alpha_next = lookup(alphas, stamp_next)
        coef_one = jnp.sqrt(alpha_next / alpha_now)
        coef_two = jnp.sqrt(1.0 - alpha_next) - coef_one * jnp.sqrt(1.0 - alpha_now)
        feats = time_features(stamp_now, time_weight.shape[1])
        embed = jnp.dot(time_weight, feats, precision=lax.Precision.HIGHEST)
        is_first = own_index == 0
        sweep_rows = []
        for sweep in range(ITERS):
            noise = denoise(current[0], embed, in_weight, mid_weight, out_weight)
            drift = (coef_one - 1.0) * current + coef_two * noise[None]
            term = drift + jnp.where(is_first, current, 0.0)
            prefix = entering(term, STEPS, add_terms, jnp.zeros_like(term))
            updated = jnp.where(is_first, current, prefix)
            sweep_rows.append(jnp.mean((updated - current) ** 2))
            current = updated
        error_rows.append(jnp.stack(sweep_rows))
        advance = advances[round_no]
        target = own_index + advance
        wanted = jnp.minimum(target, window - 1)
        block = lax.all_gather(current, STEPS, axis=0, tiled=True)
        row_ids = jnp.arange(block.shape[0], dtype=jnp.int32)
        selected = jnp.where((row_ids == wanted)[:, None, None], block, 0.0)
        current = jnp.zeros_like(current) + jnp.sum(selected, axis=0, keepdims=True)
        window_start = window_start + advance
    errors = jnp.stack(error_rows).reshape(ROUNDS, ITERS, 1)
    return (current, errors)


def solution(mesh):
    split = Mesh(
        mesh.devices.reshape(mesh.shape["groups"], 8, 8, 2),
        ("groups", "steps_0", "steps_1", "steps_2"),
    )
    in_specs = (P(GROUPS_STEPS, None, None), P("groups"), P("groups"), P(), P(), P(), P())
    out_specs = (P(GROUPS_STEPS, None, None), P("groups", None, STEPS))
    return jax.shard_map(
        shards, mesh=split, in_specs=in_specs, out_specs=out_specs, check_vma=False
    )
```

profile of v0, /device:TPU:513, one launch (start us, length us, event | category | flops | bytes accessed | tf_op | source)
XLA Modules:
  0.0 739.3 jit_solution(762342680965915315)
XLA Ops:
  30.4 22.0 %all-gather = f32[2,4,4096]{2,1,0:T(4,128)S(1)} all-gather(f32[1,4,4096]{2,1,0:T(4,128)S(1)} %fusion.34), channel_id=2, replica_groups=mesh['groups'=2,'steps_0'=8,'steps_1'=8,'steps_2'=2] {'steps_2'}, dimensions={0}, use_global_device_ids=true | all-gather | bytes 196608 | tf_op jit(solution)/shard_map/all_gather | solution.py:24
  52.5 19.3 %all-gather.8 = f32[8,4,4096]{2,1,0:T(4,128)S(1)} all-gather(f32[1,4,4096]{2,1,0:T(4,128)S(1)} %slice_add_fusion.95), channel_id=10, replica_groups=mesh['groups'=2,'steps_0'=8,'steps_1'=8,'steps_2'=2] {'steps_1'}, dimensions={0}, use_global_device_ids=true | all-gather | bytes 589824 | tf_op jit(solution)/shard_map/all_gather | solution.py:24
  71.8 19.8 %all_gather.121 = f32[8,1,4,4096]{3,2,1,0:T(4,128)S(1)} all-gather(f32[1,1,4,4096]{3,2,1,0:T(4,128)S(1)} %get-tuple-element.42), channel_id=1, replica_groups=mesh['groups'=2,'steps_0'=8,'steps_1'=8,'steps_2'=2] {'steps_0'}, dimensions={0}, use_global_device_ids=true | all-gather | bytes 589824 | tf_op jit(solution)/shard_map/all_gather | solution.py:24
  102.6 13.6 %all-gather.1 = f32[2,4,4096]{2,1,0:T(4,128)S(1)} all-gather(f32[1,4,4096]{2,1,0:T(4,128)S(1)} %fusion.31), channel_id=3, replica_groups=mesh['groups'=2,'steps_0'=8,'steps_1'=8,'steps_2'=2] {'steps_2'}, dimensions={0}, use_global_device_ids=true | all-gather | bytes 196608 | tf_op jit(solution)/shard_map/all_gather | solution.py:24
  116.3 19.3 %all-gather.9 = f32[8,4,4096]{2,1,0:T(4,128)S(1)} all-gather(f32[1,4,4096]{2,1,0:T(4,128)S(1)} %slice_add_fusion.82), channel_id=11, replica_groups=mesh['groups'=2,'steps_0'=8,'steps_1'=8,'steps_2'=2] {'steps_1'}, dimensions={0}, use_global_device_ids=true | all-gather | bytes 589824 | tf_op jit(solution)/shard_map/all_gather | solution.py:24
  135.6 19.3 %all_gather.125 = f32[8,1,4,4096]{3,2,1,0:T(4,128)S(1)} all-gather(f32[1,1,4,4096]{3,2,1,0:T(4,128)S(1)} %get-tuple-element.40), channel_id=1, replica_groups=mesh['groups'=2,'steps_0'=8,'steps_1'=8,'steps_2'=2] {'steps_0'}, dimensions={0}, use_global_device_ids=true | all-gather | bytes 589824 | tf_op jit(solution)/shard_map/all_gather | solution.py:24
  165.8 14.0 %all-gather.2 = f32[2,4,4096]{2,1,0:T(4,128)S(1)} all-gather(f32[1,4,4096]{2,1,0:T(4,128)S(1)} %fusion.28), channel_id=4, replica_groups=mesh['groups'=2,'steps_0'=8,'steps_1'=8,'steps_2'=2] {'steps_2'}, dimensions={0}, use_global_device_ids=true | all-gather | bytes 196608 | tf_op jit(solution)/shard_map/all_gather | solution.py:24
  179.9 19.3 %all-gather.10 = f32[8,4,4096]{2,1,0:T(4,128)S(1)} all-gather(f32[1,4,4096]{2,1,0:T(4,128)S(1)} %slice_add_fusion.69), channel_id=12, replica_groups=mesh['groups'=2,'steps_0'=8,'steps_1'=8,'steps_2'=2] {'steps_1'}, dimensions={0}, use_global_device_ids=true | all-gather | bytes 589824 | tf_op jit(solution)/shard_map/all_gather | solution.py:24
  199.3 19.5 %all_gather.129 = f32[8,1,4,4096]{3,2,1,0:T(4,128)S(1)} all-gather(f32[1,1,4,4096]{3,2,1,0:T(4,128)S(1)} %get-tuple-element.38), channel_id=1, replica_groups=mesh['groups'=2,'steps_0'=8,'steps_1'=8,'steps_2'=2] {'steps_0'}, dimensions={0}, use_global_device_ids=true | all-gather | bytes 589824 | tf_op jit(solution)/shard_map/all_gather | solution.py:24
  229.7 14.0 %all-gather.3 = f32[2,4,4096]{2,1,0:T(4,128)S(1)} all-gather(f32[1,4,4096]{2,1,0:T(4,128)S(1)} %fusion.25), channel_id=5, replica_groups=mesh['groups'=2,'steps_0'=8,'steps_1'=8,'steps_2'=2] {'steps_2'}, dimensions={0}, use_global_device_ids=true | all-gather | bytes 196608 | tf_op jit(solution)/shard_map/all_gather | solution.py:24
  243.7 19.6 %all-gather.11 = f32[8,4,4096]{2,1,0:T(4,128)S(1)} all-gather(f32[1,4,4096]{2,1,0:T(4,128)S(1)} %slice_add_fusion.56), channel_id=13, replica_groups=mesh['groups'=2,'steps_0'=8,'steps_1'=8,'steps_2'=2] {'steps_1'}, dimensions={0}, use_global_device_ids=true | all-gather | bytes 589824 | tf_op jit(solution)/shard_map/all_gather | solution.py:24
  263.4 19.5 %all_gather.133 = f32[8,1,4,4096]{3,2,1,0:T(4,128)S(1)} all-gather(f32[1,1,4,4096]{3,2,1,0:T(4,128)S(1)} %get-tuple-element.36), channel_id=1, replica_groups=mesh['groups'=2,'steps_0'=8,'steps_1'=8,'steps_2'=2] {'steps_0'}, dimensions={0}, use_global_device_ids=true | all-gather | bytes 589824 | tf_op jit(solution)/shard_map/all_gather | solution.py:24
  288.8 91.7 %all-gather.27.cloned.1.call-done = f32[128,4,4096]{2,1,0:T(4,128)} async-done(((f32[1,4,4096]{2,1,0:T(4,128)}), f32[128,4,4096]{2,1,0:T(4,128)}) %all-gather.27.cloned.1.call-update) | async-done | bytes 8388624 | tf_op jit(solution)/shard_map/all_gather | solution.py:99
  399.1 19.9 %all-gather.17 = f32[8,4,4096]{2,1,0:T(4,128)S(1)} all-gather(f32[1,4,4096]{2,1,0:T(4,128)S(1)} %slice_add_fusion.43), channel_id=14, replica_groups=mesh['groups'=2,'steps_0'=8,'steps_1'=8,'steps_2'=2] {'steps_1'}, dimensions={0}, use_global_device_ids=true | all-gather | bytes 589824 | tf_op jit(solution)/shard_map/all_gather | solution.py:24
  419.0 20.6 %all_gather.138 = f32[8,1,4,4096]{3,2,1,0:T(4,128)S(1)} all-gather(f32[1,1,4,4096]{3,2,1,0:T(4,128)S(1)} %get-tuple-element.34), channel_id=1, replica_groups=mesh['groups'=2,'steps_0'=8,'steps_1'=8,'steps_2'=2] {'steps_0'}, dimensions={0}, use_global_device_ids=true | all-gather | bytes 589824 | tf_op jit(solution)/shard_map/all_gather | solution.py:24
  463.2 19.3 %all-gather.19 = f32[8,4,4096]{2,1,0:T(4,128)S(1)} all-gather(f32[1,4,4096]{2,1,0:T(4,128)S(1)} %slice_add_fusion.32), channel_id=15, replica_groups=mesh['groups'=2,'steps_0'=8,'steps_1'=8,'steps_2'=2] {'steps_1'}, dimensions={0}, use_global_device_ids=true | all-gather | bytes 589824 | tf_op jit(solution)/shard_map/all_gather | solution.py:24
  482.6 19.4 %all_gather.142 = f32[8,1,4,4096]{3,2,1,0:T(4,128)S(1)} all-gather(f32[1,1,4,4096]{3,2,1,0:T(4,128)S(1)} %get-tuple-element.30), channel_id=1, replica_groups=mesh['groups'=2,'steps_0'=8,'steps_1'=8,'steps_2'=2] {'steps_0'}, dimensions={0}, use_global_device_ids=true | all-gather | bytes 589824 | tf_op jit(solution)/shard_map/all_gather | solution.py:24
  513.0 14.3 %all-gather.20 = f32[2,4,4096]{2,1,0:T(4,128)S(1)} all-gather(f32[1,4,4096]{2,1,0:T(4,128)S(1)} %fusion.14), channel_id=8, replica_groups=mesh['groups'=2,'steps_0'=8,'steps_1'=8,'steps_2'=2] {'steps_2'}, dimensions={0}, use_global_device_ids=true | all-gather | bytes 196608 | tf_op jit(solution)/shard_map/all_gather | solution.py:24
  527.3 20.1 %all-gather.21 = f32[8,4,4096]{2,1,0:T(4,128)S(1)} all-gather(f32[1,4,4096]{2,1,0:T(4,128)S(1)} %slice_add_fusion.21), channel_id=16, replica_groups=mesh['groups'=2,'steps_0'=8,'steps_1'=8,'steps_2'=2] {'steps_1'}, dimensions={0}, use_global_device_ids=true | all-gather | bytes 589824 | tf_op jit(solution)/shard_map/all_gather | solution.py:24
  547.4 19.4 %all_gather.146 = f32[8,1,4,4096]{3,2,1,0:T(4,128)S(1)} all-gather(f32[1,1,4,4096]{3,2,1,0:T(4,128)S(1)} %get-tuple-element.26), channel_id=1, replica_groups=mesh['groups'=2,'steps_0'=8,'steps_1'=8,'steps_2'=2] {'steps_0'}, dimensions={0}, use_global_device_ids=true | all-gather | bytes 589824 | tf_op jit(solution)/shard_map/all_gather | solution.py:24
  577.7 13.6 %all-gather.22 = f32[2,4,4096]{2,1,0:T(4,128)S(1)} all-gather(f32[1,4,4096]{2,1,0:T(4,128)S(1)} %fusion.10), channel_id=9, replica_groups=mesh['groups'=2,'steps_0'=8,'steps_1'=8,'steps_2'=2] {'steps_2'}, dimensions={0}, use_global_device_ids=true | all-gather | bytes 196608 | tf_op jit(solution)/shard_map/all_gather | solution.py:24
  591.3 19.9 %all-gather.23 = f32[8,4,4096]{2,1,0:T(4,128)S(1)} all-gather(f32[1,4,4096]{2,1,0:T(4,128)S(1)} %slice_add_fusion.10), channel_id=17, replica_groups=mesh['groups'=2,'steps_0'=8,'steps_1'=8,'steps_2'=2] {'steps_1'}, dimensions={0}, use_global_device_ids=true | all-gather | bytes 589824 | tf_op jit(solution)/shard_map/all_gather | solution.py:24
  611.3 19.3 %all_gather.150 = f32[8,1,4,4096]{3,2,1,0:T(4,128)S(1)} all-gather(f32[1,1,4,4096]{3,2,1,0:T(4,128)S(1)} %get-tuple-element.22), channel_id=1, replica_groups=mesh['groups'=2,'steps_0'=8,'steps_1'=8,'steps_2'=2] {'steps_0'}, dimensions={0}, use_global_device_ids=true | all-gather | bytes 589824 | tf_op jit(solution)/shard_map/all_gather | solution.py:24
  638.5 87.3 %all-gather.29.cloned.1.call-done = f32[128,4,4096]{2,1,0:T(4,128)} async-done(((f32[1,4,4096]{2,1,0:T(4,128)}), f32[128,4,4096]{2,1,0:T(4,128)}) %all-gather.29.cloned.1.call-update) | async-done | bytes 8388624 | tf_op jit(solution)/shard_map/all_gather | solution.py:99
  (84 shorter events, 127.8 us)
Async XLA Ops:
  7.2 11.0 %copy-start = (f32[320,320]{1,0:T(8,128)S(1)}, f32[320,320]{1,0:T(8,128)}, u32[]{:S(2)}) copy-start(f32[320,320]{1,0:T(8,128)} %param.11) | copy-start | bytes 1228804
  7.2 15.7 %copy-start.2 = (f32[1,4,4096]{2,1,0:T(4,128)S(1)}, f32[1,4,4096]{2,1,0:T(4,128)}, u32[]{:S(2)}) copy-start(f32[1,4,4096]{2,1,0:T(4,128)} %param.7) | copy-start | bytes 196612
  7.2 15.7 %copy-start.4 = (bf16[320,320]{1,0:T(8,128)(2,1)S(1)}, bf16[320,320]{1,0:T(8,128)(2,1)}, u32[]{:S(2)}) copy-start(bf16[320,320]{1,0:T(8,128)(2,1)} %param.12) | copy-start | bytes 614404
  7.2 15.7 %copy-start.5 = (bf16[4,320]{1,0:T(4,128)(2,1)S(1)}, bf16[4,320]{1,0:T(4,128)(2,1)}, u32[]{:S(2)}) copy-start(bf16[4,320]{1,0:T(4,128)(2,1)} %param.13) | copy-start | bytes 7684
  7.2 373.3 %all-gather.27.cloned.1.call-start = ((), (), s32[]{:S(2)}) async-start(), calls=%async_computation | async-start | bytes 8454144 | tf_op jit(solution)/shard_map/all_gather | solution.py:99
  22.9 69.0 %copy-start.3 = (bf16[320,4]{0,1:T(4,128)(2,1)S(1)}, bf16[320,4]{0,1:T(4,128)(2,1)}, u32[]{:S(2)}) copy-start(bf16[320,4]{0,1:T(4,128)(2,1)} %param.10) | copy-start | bytes 7684
  284.4 441.4 %all-gather.29.cloned.1.call-start = ((), (), s32[]{:S(2)}) async-start(), calls=%async_computation.1 | async-start | bytes 8454144 | tf_op jit(solution)/shard_map/all_gather | solution.py:99
  630.6 101.7 %copy-start.1 = (f32[320,320]{1,0:T(8,128)S(1)}, f32[320,320]{1,0:T(8,128)}, u32[]{:S(2)}) copy-start(f32[320,320]{1,0:T(8,128)} %param.11) | copy-start | bytes 1228804
Sparse Core Ops, SparseCore 0:
  284.6 95.8 all-gather.26
  632.4 93.3 all-gather.28
where the time goes:
time: 748 us; the launch traced here: 739 us
  blocking collectives  420 us (56%)
  waiting for transfers between devices  179 us (24%)
  matrix products  88 us (12%)
  between operations  27.5 us (4%)
  other arithmetic  21.6 us (3%)
    all_gather x24, blocking collectives, entering(): pieces = lax.all_gather(so_far, axis)  420 us
    all_gather x2, waiting for transfers between devices, shards(): block = lax.all_gather(current, STEPS, axis=0, tiled=True)  179 us
    dot_general x8, matrix products, denoise(): return jnp.dot(out_weight, hidden_two, preferred_element_type=jnp.float32)  60.3 us
    dot_general x8, matrix products, denoise(): jnp.dot(in_weight, state.astype(jnp.bfloat16), preferred_element_type=jnp...  26.6 us
  transfers between devices with their start and end apart: 2, of which 2 were waited for; matrix products, arithmetic and copies ran while one was open for 0% of the time, Pallas kernels for 0%

commit v1 on v0

--- a/solution.py
+++ b/solution.py
@@ -96,7 +96,10 @@
         advance = advances[round_no]
         target = own_index + advance
         wanted = jnp.minimum(target, window - 1)
-        block = lax.all_gather(current, STEPS, axis=0, tiled=True)
+        clean = lax.axis_size(STEPS)
+        lower = jnp.stack([current] * clean, 0)
+        ready = lax.all_to_all(lower, split_axis=0, axis_name=STEPS, concat_axis=0)
+        block = jnp.concatenate(ready, 0)
         row_ids = jnp.arange(block.shape[0], dtype=jnp.int32)
         selected = jnp.where((row_ids == wanted)[:, None, None], block, 0.0)
         current = jnp.zeros_like(current) + jnp.sum(selected, axis=0, keepdims=True)

time: 748 us -> 1080 us (1.44)
  the two profiles are of different devices: /device:TPU:513 before, /device:TPU:553 now
where the time goes in v1:
time: 1080 us
  waiting for transfers between devices  472 us (44%)
  blocking collectives  413 us (38%)
  matrix products  88 us (8%)
  starting transfers between devices  53.9 us (5%)
  other arithmetic  20.5 us (2%)
  between operations  14.3 us (1%)
  local copies, waits for them, and re-layouts  13.7 us (1%)
    all_to_all x2, waiting for transfers between devices, shards(): ready = lax.all_to_all(lower, split_axis=0, axis_name=STEPS, concat_axis=0)  472 us
    all_gather x24, blocking collectives, entering(): pieces = lax.all_gather(so_far, axis)  413 us
    dot_general x8, matrix products, denoise(): return jnp.dot(out_weight, hidden_two, preferred_element_type=jnp.float32)  60.3 us
    all_to_all x2, starting transfers between devices, shards(): ready = lax.all_to_all(lower, split_axis=0, axis_name=STEPS, concat_axis=0)  53.9 us
    dot_general x8, matrix products, denoise(): jnp.dot(in_weight, state.astype(jnp.bfloat16), preferred_element_type=jnp...  26.6 us
  transfers between devices with their start and end apart: 2, of which 2 were waited for; matrix products, arithmetic and copies ran while one was open for 0% of the time, Pallas kernels for 0%

profile of v1, /device:TPU:553, one launch (start us, length us, event | category | flops | bytes accessed | tf_op | source)
XLA Modules:
  0.0 1075.5 jit_solution(3037626748209976962)
XLA Ops:
  26.1 19.4 %all-gather.8 = f32[8,4,4096]{2,1,0:T(4,128)S(1)} all-gather(f32[1,4,4096]{2,1,0:T(4,128)S(1)} %slice_add_fusion.95), channel_id=10, replica_groups=mesh['groups'=2,'steps_0'=8,'steps_1'=8,'steps_2'=2] {'steps_1'}, dimensions={0}, use_global_device_ids=true | all-gather | bytes 589824 | tf_op jit(solution)/shard_map/all_gather | solution.py:24
  45.6 29.1 %all_gather.115 = f32[8,1,4,4096]{3,2,1,0:T(4,128)S(1)} all-gather(f32[1,1,4,4096]{3,2,1,0:T(4,128)S(1)} %get-tuple-element.42), channel_id=1, replica_groups=mesh['groups'=2,'steps_0'=8,'steps_1'=8,'steps_2'=2] {'steps_0'}, dimensions={0}, use_global_device_ids=true | all-gather | bytes 589824 | tf_op jit(solution)/shard_map/all_gather | solution.py:24
  85.6 13.5 %all-gather.1 = f32[2,4,4096]{2,1,0:T(4,128)S(1)} all-gather(f32[1,4,4096]{2,1,0:T(4,128)S(1)} %fusion.33), channel_id=3, replica_groups=mesh['groups'=2,'steps_0'=8,'steps_1'=8,'steps_2'=2] {'steps_2'}, dimensions={0}, use_global_device_ids=true | all-gather | bytes 196608 | tf_op jit(solution)/shard_map/all_gather | solution.py:24
  99.2 20.1 %all-gather.9 = f32[8,4,4096]{2,1,0:T(4,128)S(1)} all-gather(f32[1,4,4096]{2,1,0:T(4,128)S(1)} %slice_add_fusion.82), channel_id=11, replica_groups=mesh['groups'=2,'steps_0'=8,'steps_1'=8,'steps_2'=2] {'steps_1'}, dimensions={0}, use_global_device_ids=true | all-gather | bytes 589824 | tf_op jit(solution)/shard_map/all_gather | solution.py:24
  119.3 19.8 %all_gather.119 = f32[8,1,4,4096]{3,2,1,0:T(4,128)S(1)} all-gather(f32[1,1,4,4096]{3,2,1,0:T(4,128)S(1)} %get-tuple-element.40), channel_id=1, replica_groups=mesh['groups'=2,'steps_0'=8,'steps_1'=8,'steps_2'=2] {'steps_0'}, dimensions={0}, use_global_device_ids=true | all-gather | bytes 589824 | tf_op jit(solution)/shard_map/all_gather | solution.py:24
  163.1 19.8 %all-gather.10 = f32[8,4,4096]{2,1,0:T(4,128)S(1)} all-gather(f32[1,4,4096]{2,1,0:T(4,128)S(1)} %slice_add_fusion.69), channel_id=12, replica_groups=mesh['groups'=2,'steps_0'=8,'steps_1'=8,'steps_2'=2] {'steps_1'}, dimensions={0}, use_global_device_ids=true | all-gather | bytes 589824 | tf_op jit(solution)/shard_map/all_gather | solution.py:24
  183.0 20.3 %all_gather.123 = f32[8,1,4,4096]{3,2,1,0:T(4,128)S(1)} all-gather(f32[1,1,4,4096]{3,2,1,0:T(4,128)S(1)} %get-tuple-element.38), channel_id=1, replica_groups=mesh['groups'=2,'steps_0'=8,'steps_1'=8,'steps_2'=2] {'steps_0'}, dimensions={0}, use_global_device_ids=true | all-gather | bytes 589824 | tf_op jit(solution)/shard_map/all_gather | solution.py:24
  227.5 19.8 %all-gather.11 = f32[8,4,4096]{2,1,0:T(4,128)S(1)} all-gather(f32[1,4,4096]{2,1,0:T(4,128)S(1)} %slice_add_fusion.56), channel_id=13, replica_groups=mesh['groups'=2,'steps_0'=8,'steps_1'=8,'steps_2'=2] {'steps_1'}, dimensions={0}, use_global_device_ids=true | all-gather | bytes 589824 | tf_op jit(solution)/shard_map/all_gather | solution.py:24
  247.3 19.8 %all_gather.127 = f32[8,1,4,4096]{3,2,1,0:T(4,128)S(1)} all-gather(f32[1,1,4,4096]{3,2,1,0:T(4,128)S(1)} %get-tuple-element.36), channel_id=1, replica_groups=mesh['groups'=2,'steps_0'=8,'steps_1'=8,'steps_2'=2] {'steps_0'}, dimensions={0}, use_global_device_ids=true | all-gather | bytes 589824 | tf_op jit(solution)/shard_map/all_gather | solution.py:24
  273.4 26.5 %all-to-all-start = ((f32[128,1,4,4096]{3,2,1,0:T(4,128)}), f32[128,1,4,4096]{3,2,1,0:T(4,128)}, u32[]{:S(2)}, u32[]{:S(2)}) async-start(f32[128,1,4,4096]{3,2,1,0:T(4,128)} %stack.32), calls=%async_computation | async-start | bytes 16777216 | tf_op jit(solution)/shard_map/all_to_all | solution.py:101
  303.9 231.9 %all-to-all-done = f32[128,1,4,4096]{3,2,1,0:T(4,128)} async-done(((f32[128,1,4,4096]{3,2,1,0:T(4,128)}), f32[128,1,4,4096]{3,2,1,0:T(4,128)}, u32[]{:S(2)}, u32[]{:S(2)}) %all-to-all-start) | async-done | bytes 8388640 | tf_op jit(solution)/shard_map/all_to_all | solution.py:101
  554.3 19.4 %all-gather.17 = f32[8,4,4096]{2,1,0:T(4,128)S(1)} all-gather(f32[1,4,4096]{2,1,0:T(4,128)S(1)} %slice_add_fusion.43), channel_id=14, replica_groups=mesh['groups'=2,'steps_0'=8,'steps_1'=8,'steps_2'=2] {'steps_1'}, dimensions={0}, use_global_device_ids=true | all-gather | bytes 589824 | tf_op jit(solution)/shard_map/all_gather | solution.py:24
  573.8 23.4 %all_gather.131 = f32[8,1,4,4096]{3,2,1,0:T(4,128)S(1)} all-gather(f32[1,1,4,4096]{3,2,1,0:T(4,128)S(1)} %get-tuple-element.34), channel_id=1, replica_groups=mesh['groups'=2,'steps_0'=8,'steps_1'=8,'steps_2'=2] {'steps_0'}, dimensions={0}, use_global_device_ids=true | all-gather | bytes 589824 | tf_op jit(solution)/shard_map/all_gather | solution.py:24
  608.1 14.2 %all-gather.18 = f32[2,4,4096]{2,1,0:T(4,128)S(1)} all-gather(f32[1,4,4096]{2,1,0:T(4,128)S(1)} %fusion.20), channel_id=7, replica_groups=mesh['groups'=2,'steps_0'=8,'steps_1'=8,'steps_2'=2] {'steps_2'}, dimensions={0}, use_global_device_ids=true | all-gather | bytes 196608 | tf_op jit(solution)/shard_map/all_gather | solution.py:24
  622.2 19.8 %all-gather.19 = f32[8,4,4096]{2,1,0:T(4,128)S(1)} all-gather(f32[1,4,4096]{2,1,0:T(4,128)S(1)} %slice_add_fusion.32), channel_id=15, replica_groups=mesh['groups'=2,'steps_0'=8,'steps_1'=8,'steps_2'=2] {'steps_1'}, dimensions={0}, use_global_device_ids=true | all-gather | bytes 589824 | tf_op jit(solution)/shard_map/all_gather | solution.py:24
  642.1 18.9 %all_gather.135 = f32[8,1,4,4096]{3,2,1,0:T(4,128)S(1)} all-gather(f32[1,1,4,4096]{3,2,1,0:T(4,128)S(1)} %get-tuple-element.30), channel_id=1, replica_groups=mesh['groups'=2,'steps_0'=8,'steps_1'=8,'steps_2'=2] {'steps_0'}, dimensions={0}, use_global_device_ids=true | all-gather | bytes 589824 | tf_op jit(solution)/shard_map/all_gather | solution.py:24
  672.0 14.0 %all-gather.20 = f32[2,4,4096]{2,1,0:T(4,128)S(1)} all-gather(f32[1,4,4096]{2,1,0:T(4,128)S(1)} %fusion.16), channel_id=8, replica_groups=mesh['groups'=2,'steps_0'=8,'steps_1'=8,'steps_2'=2] {'steps_2'}, dimensions={0}, use_global_device_ids=true | all-gather | bytes 196608 | tf_op jit(solution)/shard_map/all_gather | solution.py:24
  686.0 19.9 %all-gather.21 = f32[8,4,4096]{2,1,0:T(4,128)S(1)} all-gather(f32[1,4,4096]{2,1,0:T(4,128)S(1)} %slice_add_fusion.21), channel_id=16, replica_groups=mesh['groups'=2,'steps_0'=8,'steps_1'=8,'steps_2'=2] {'steps_1'}, dimensions={0}, use_global_device_ids=true | all-gather | bytes 589824 | tf_op jit(solution)/shard_map/all_gather | solution.py:24
  705.9 19.1 %all_gather.139 = f32[8,1,4,4096]{3,2,1,0:T(4,128)S(1)} all-gather(f32[1,1,4,4096]{3,2,1,0:T(4,128)S(1)} %get-tuple-element.26), channel_id=1, replica_groups=mesh['groups'=2,'steps_0'=8,'steps_1'=8,'steps_2'=2] {'steps_0'}, dimensions={0}, use_global_device_ids=true | all-gather | bytes 589824 | tf_op jit(solution)/shard_map/all_gather | solution.py:24
  735.9 14.1 %all-gather.22 = f32[2,4,4096]{2,1,0:T(4,128)S(1)} all-gather(f32[1,4,4096]{2,1,0:T(4,128)S(1)} %fusion.12), channel_id=9, replica_groups=mesh['groups'=2,'steps_0'=8,'steps_1'=8,'steps_2'=2] {'steps_2'}, dimensions={0}, use_global_device_ids=true | all-gather | bytes 196608 | tf_op jit(solution)/shard_map/all_gather | solution.py:24
  750.0 19.4 %all-gather.23 = f32[8,4,4096]{2,1,0:T(4,128)S(1)} all-gather(f32[1,4,4096]{2,1,0:T(4,128)S(1)} %slice_add_fusion.10), channel_id=17, replica_groups=mesh['groups'=2,'steps_0'=8,'steps_1'=8,'steps_2'=2] {'steps_1'}, dimensions={0}, use_global_device_ids=true | all-gather | bytes 589824 | tf_op jit(solution)/shard_map/all_gather | solution.py:24
  769.5 19.3 %all_gather.143 = f32[8,1,4,4096]{3,2,1,0:T(4,128)S(1)} all-gather(f32[1,1,4,4096]{3,2,1,0:T(4,128)S(1)} %get-tuple-element.22), channel_id=1, replica_groups=mesh['groups'=2,'steps_0'=8,'steps_1'=8,'steps_2'=2] {'steps_0'}, dimensions={0}, use_global_device_ids=true | all-gather | bytes 589824 | tf_op jit(solution)/shard_map/all_gather | solution.py:24
  794.9 27.4 %all-to-all-start.1 = ((f32[128,1,4,4096]{3,2,1,0:T(4,128)}), f32[128,1,4,4096]{3,2,1,0:T(4,128)}, u32[]{:S(2)}, u32[]{:S(2)}) async-start(f32[128,1,4,4096]{3,2,1,0:T(4,128)} %stack.34), calls=%async_computation.1 | async-start | bytes 16777216 | tf_op jit(solution)/shard_map/all_to_all | solution.py:101
  828.9 239.9 %all-to-all-done.1 = f32[128,1,4,4096]{3,2,1,0:T(4,128)} async-done(((f32[128,1,4,4096]{3,2,1,0:T(4,128)}), f32[128,1,4,4096]{3,2,1,0:T(4,128)}, u32[]{:S(2)}, u32[]{:S(2)}) %all-to-all-start.1) | async-done | bytes 8388640 | tf_op jit(solution)/shard_map/all_to_all | solution.py:101
  (84 shorter events, 152.6 us)
Async XLA Ops:
  0.6 11.0 %copy-start = (f32[320,320]{1,0:T(8,128)S(1)}, f32[320,320]{1,0:T(8,128)}, u32[]{:S(2)}) copy-start(f32[320,320]{1,0:T(8,128)} %param.11) | copy-start | bytes 1228804
  0.6 15.7 %copy-start.2 = (f32[1,4,4096]{2,1,0:T(4,128)S(1)}, f32[1,4,4096]{2,1,0:T(4,128)}, u32[]{:S(2)}) copy-start(f32[1,4,4096]{2,1,0:T(4,128)} %param.7) | copy-start | bytes 196612
  0.7 15.7 %copy-start.4 = (bf16[320,320]{1,0:T(8,128)(2,1)S(1)}, bf16[320,320]{1,0:T(8,128)(2,1)}, u32[]{:S(2)}) copy-start(bf16[320,320]{1,0:T(8,128)(2,1)} %param.12) | copy-start | bytes 614404
  0.7 15.7 %copy-start.5 = (bf16[4,320]{1,0:T(4,128)(2,1)S(1)}, bf16[4,320]{1,0:T(4,128)(2,1)}, u32[]{:S(2)}) copy-start(bf16[4,320]{1,0:T(4,128)(2,1)} %param.13) | copy-start | bytes 7684
  16.3 58.5 %copy-start.3 = (bf16[320,4]{0,1:T(4,128)(2,1)S(1)}, bf16[320,4]{0,1:T(4,128)(2,1)}, u32[]{:S(2)}) copy-start(bf16[320,4]{0,1:T(4,128)(2,1)} %param.10) | copy-start | bytes 7684
  273.4 262.4 %all-to-all-start = ((f32[128,1,4,4096]{3,2,1,0:T(4,128)}), f32[128,1,4,4096]{3,2,1,0:T(4,128)}, u32[]{:S(2)}, u32[]{:S(2)}) async-start(f32[128,1,4,4096]{3,2,1,0:T(4,128)} %stack.32), calls=%async_computation | async-start | bytes 16777216 | tf_op jit(solution)/shard_map/all_to_all | solution.py:101
  794.9 273.9 %all-to-all-start.1 = ((f32[128,1,4,4096]{3,2,1,0:T(4,128)}), f32[128,1,4,4096]{3,2,1,0:T(4,128)}, u32[]{:S(2)}, u32[]{:S(2)}) async-start(f32[128,1,4,4096]{3,2,1,0:T(4,128)} %stack.34), calls=%async_computation.1 | async-start | bytes 16777216 | tf_op jit(solution)/shard_map/all_to_all | solution.py:101
  822.4 253.0 %copy-start.1 = (f32[320,320]{1,0:T(8,128)S(1)}, f32[320,320]{1,0:T(8,128)}, u32[]{:S(2)}) copy-start(f32[320,320]{1,0:T(8,128)} %param.11) | copy-start | bytes 1228804
